TPU v7x, 128 devices: a whole 4x4x4 slice. The times are simulated.
128 devices in a mesh: tm: 8 (over y, core), ep: 16 (over x, z).
Axes of the slice: x: 4, y: 4, z: 4, core: 2. Of those that a mesh axis runs over, the one named last changes fastest.
Arguments:
- observations: bfloat16 [1024, 128, 1024], P('ep', 'tm'), may hold values from -6 to 6
- input_weight: bfloat16 [1024, 2048], replicated, may hold values from -0.1875 to 0.1875
- hidden_weight: bfloat16 [512, 2048], replicated, may hold values from -0.25 to 0.25
- gate_bias: float32 [2048], replicated, may hold values from -3 to 3
- forget_bias: float32 [512], replicated, may hold values from 0 to 5
- episode_ids: int32 [2048], P('ep'), may hold values from 0 to 63
- start_steps: int32 [2048], P('ep'), may hold values from 0 to 127
- priorities: int32 [2048], P('ep'), may hold values from 20 to 999
Outputs:
- train_rows: bfloat16 [2048, 128, 1024], P('ep', 'tm')
- start_state: bfloat16 [2048, 2, 512], P('ep')
- sample_weights: bfloat16 [2048], P('ep')
Inputs may be any that keep to these rules, and one draw needn't show every extreme that they name: `episode_ids`: slot index inside the storage shard that sampled the sequence.
All inputs are finite; a program needn't handle non-finite values.
Results may differ from a plain program's by a relative error of at most 0.009.
Values may be sent and summed in bfloat16 or wider, within the bound.
No kernel may reach another device: no remote copies, remote signals or barrier semaphores. Data moves between devices by JAX's collectives and lax.ppermute only.
A program may use at most 64 MiB of HBM per device.

v0:
```python
import jax
import jax.numpy as jnp
from jax import lax
from jax.sharding import Mesh
from jax.sharding import PartitionSpec as P

STEPS = 128
BURN = 40
UNROLL = 80
EP = ("ep_0", "ep_1")
IMPORTANCE = 0.6


def split_up(x, dim, devices):
    before, after = (x.shape[:dim], x.shape[dim + 1 :])
    return jnp.moveaxis(x.reshape(*before, devices, -1, *after), dim, 0)


def sum_at_owner(x, axis, dim):
    devices = lax.axis_size(axis)
    tiles = lax.all_to_all(split_up(x, dim, devices), axis, 0, 0, tiled=True)
    return jnp.sum(tiles.astype(jnp.float32), axis=0)


def one_axis_at_a_time(x, axes):
    for axis in axes:
        x = lax.pmax(x, axis)
    return x


def sent_together(arrays, axis, split_dim, concat_dim, along):
    columns = [a.reshape(*a.shape[:along], -1) for a in arrays]
    both = jnp.concatenate(columns, axis=along)
    whole, at, gathered = (
        lax.all_to_all(both, axis, split_axis=split_dim, concat_axis=concat_dim, tiled=True),
        0,
        [],
    )
    for a, column in zip(arrays, columns):
        piece = whole[..., at : at + column.shape[along]]
        gathered.append(piece.reshape(*piece.shape[:along], *a.shape[along:]))
        at += column.shape[along]
    return tuple(gathered)


def joined_along(tiles, dim):
    tiles = jnp.moveaxis(tiles, 0, dim)
    lengths = tiles.shape
    return tiles.reshape(*lengths[:dim], lengths[dim] * lengths[dim + 1], *lengths[dim + 2 :])


def sent_to_all(x, axis):
    copies = jnp.broadcast_to(x, (lax.axis_size(axis), *x.shape))
    return lax.all_to_all(copies, axis, split_axis=0, concat_axis=0, tiled=True)


def collect(x, axis, dim):
    return joined_along(sent_to_all(x, axis), dim)


def lstm_step(state_pair, projected, hidden_weight, gate_bias, forget_bias):
    hidden, cell_state = state_pair
    hidden_width = hidden.shape[-1]
    gate_sum = (
        projected
        + jnp.dot(hidden.astype(jnp.bfloat16), hidden_weight, preferred_element_type=jnp.float32)
        + gate_bias
    )
    ingate = gate_sum[:, :hidden_width]
    forget = gate_sum[:, hidden_width : 2 * hidden_width]
    candidate = gate_sum[:, 2 * hidden_width : 3 * hidden_width]
    outgate = gate_sum[:, 3 * hidden_width :]
    cell_state = jax.nn.sigmoid(forget + forget_bias) * cell_state + jax.nn.sigmoid(
        ingate
    ) * jnp.tanh(candidate)
    hidden = jax.nn.sigmoid(outgate) * jnp.tanh(cell_state)
    return (hidden, cell_state)


def body(
    observations,
    input_weight,
    hidden_weight,
    gate_bias,
    forget_bias,
    episode_ids,
    start_steps,
    priorities,
):
    shard_steps = observations.shape[1]
    seq_count = episode_ids.shape[0]
    hidden_width = hidden_weight.shape[0]
    time_shards = lax.axis_size("tm")
    position = lax.axis_index("tm")
    stored_rows = observations[episode_ids]
    local_steps = position * shard_steps + jnp.arange(shard_steps, dtype=jnp.int32)
    offsets = (local_steps[None, :] - start_steps[:, None]) % STEPS
    own_count = seq_count // time_shards
    whole_slots = lax.all_to_all(stored_rows, "tm", split_axis=0, concat_axis=1, tiled=True)
    own_starts = lax.dynamic_slice_in_dim(start_steps, position * own_count, own_count)
    burn_steps = (own_starts[None, :] + jnp.arange(BURN, dtype=jnp.int32)[:, None]) % STEPS
    own_index = jnp.broadcast_to(jnp.arange(own_count, dtype=jnp.int32)[None, :], burn_steps.shape)
    burn_inputs = whole_slots[own_index, burn_steps]
    burn_projected = jnp.dot(
        burn_inputs.reshape(BURN * own_count, burn_inputs.shape[2]),
        input_weight,
        preferred_element_type=jnp.float32,
    ).reshape(BURN, own_count, -1)

    def warm(state_pair, projected_now):
        return (lstm_step(state_pair, projected_now, hidden_weight, gate_bias, forget_bias), None)

    blank_own = jnp.zeros((own_count, hidden_width), jnp.float32)
    (own_hidden, own_cell), _ = lax.scan(warm, (blank_own, blank_own), burn_projected, unroll=4)
    own_pair = jnp.stack([own_hidden, own_cell], axis=1)
    final_pair = lax.dynamic_update_slice_in_dim(
        jnp.zeros((seq_count, 2, hidden_width), jnp.float32), own_pair, position * own_count, 0
    )
    start_state = sum_at_owner(final_pair.astype(jnp.bfloat16), "tm", 2).astype(jnp.bfloat16)
    train_mask = (offsets - BURN) % STEPS < UNROLL
    sent_rows = jnp.where(train_mask[:, :, None], stored_rows, jnp.zeros((), jnp.bfloat16))
    raw_weight = jnp.exp(-IMPORTANCE * jnp.log(priorities.astype(jnp.float32))).astype(jnp.bfloat16)
    peak_weight = one_axis_at_a_time(jnp.max(raw_weight.astype(jnp.float32)), EP)
    outgoing = (raw_weight.astype(jnp.float32) / peak_weight).astype(jnp.bfloat16)
    moved_rows, moved_state, moved_weights = sent_together(
        (sent_rows, start_state, outgoing), EP, 0, 0, 1
    )
    moved_state = collect(moved_state, "tm", 2)
    return (moved_rows, moved_state, moved_weights)


def solution(mesh):
    torus = Mesh(mesh.devices.reshape(mesh.shape["tm"], 4, 4), ("tm", "ep_0", "ep_1"))
    return jax.shard_map(
        body,
        mesh=torus,
        in_specs=(P(EP, "tm", None), P(), P(), P(), P(), P(EP), P(EP), P(EP)),
        out_specs=(P(EP, "tm", None), P(EP, None, None), P(EP)),
        check_vma=False,
    )
```

profile of v0, /device:TPU:1, one launch (start us, length us, event | category | flops | bytes accessed | tf_op | source)
XLA Modules:
  0.0 274.5 jit_solution(11965095968492109559)
XLA Ops:
  2.2 2.8 %gather_fusion = bf16[128,16,1024]{2,1,0:T(8,128)(2,1)} fusion(bf16[64,16,1024]{2,1,0:T(8,128)(2,1)S(1)} %copy-done, s32[1024]{0:T(1024)S(1)} %pad_clamp_fusion), kind=kCustom, calls=%fused_computation | custom fusion | bytes 8389120 | tf_op jit(solution)/shard_map/gather | solution.py:95
  5.1 6.1 %all-to-all-start = ((bf16[128,16,1024]{2,1,0:T(8,128)(2,1)}), bf16[128,16,1024]{2,1,0:T(8,128)(2,1)}, u32[]{:S(2)}, u32[]{:S(2)}) async-start(bf16[128,16,1024]{2,1,0:T(8,128)(2,1)} %gather_fusion), calls=%async_computation | async-start | bytes 8388608 | tf_op jit(solution)/shard_map/all_to_all | solution.py:99
  11.8 10.0 %pmax.14 = f32[]{:T(128)} all-reduce(bf16[]{:T(256)} %convert_reduce_fusion), channel_id=1, replica_groups=mesh['tm'=8,'ep_0'=4,'ep_1'=4] {'ep_0'}, use_global_device_ids=true, to_apply=%region_4.5 | all-reduce | flops 1 | bytes 6 | tf_op jit(solution)/shard_map/pmax | solution.py:27
  22.1 37.9 %all-to-all-done = bf16[128,16,1024]{2,1,0:T(8,128)(2,1)} async-done(((bf16[128,16,1024]{2,1,0:T(8,128)(2,1)}), bf16[128,16,1024]{2,1,0:T(8,128)(2,1)}, u32[]{:S(2)}, u32[]{:S(2)}) %all-to-all-start) | async-done | bytes 4194336 | tf_op jit(solution)/shard_map/all_to_all | solution.py:99
  59.9 5.0 %copy.28 = bf16[8,16,16,1024]{3,2,0,1:T(8,128)(2,1)} copy(bf16[8,16,16,1024]{3,2,1,0:T(8,128)(2,1)} %bitcast) | data formatting | bytes 8388608 | tf_op jit(solution)/shard_map/all_to_all | solution.py:99
  64.9 15.3 %gather_fusion.1 = bf16[640,1024]{1,0:T(8,128)(2,1)} fusion(bf16[16,128,1024]{2,1,0:T(8,128)(2,1)} %bitcast.61, s32[640]{0:T(1024)S(1)} %reshape.199), kind=kCustom, calls=%fused_computation.1 | custom fusion | bytes 2626560 | tf_op jit(solution)/shard_map/gather | solution.py:103
  80.3 7.8 %fusion.75 = f32[10,4,16,2048]{3,2,1,0:T(8,128)} fusion(bf16[10,4,16,1024]{3,2,1,0:T(8,128)(2,1)} %bitcast.67, bf16[1024,2048]{1,0:T(8,128)(2,1)} %param.11), kind=kOutput, calls=%fused_computation.100 | convolution fusion | flops 2684354560 | bytes 10747904 | tf_op jit(solution)/shard_map/dot_general | solution.py:104
  88.1 81.5 %while.13 = (s32[]{:T(128)}, bf16[16,512]{1,0:T(8,128)(2,1)S(1)}, f32[16,512]{1,0:T(8,128)S(1)}, f32[10,4,16,2048]{3,2,1,0:T(8,128)}, bf16[512,2048]{1,0:T(8,128...) while((s32[]{:T(128)}, bf16[16,512]{1,0:T(8,128)(2,1)S(1)}, ...), condition=%wide.region_1.2_spmd.clone, body=%wide.region_0.1_spmd.clone.sunk | while | flops 134987776 | bytes 10395840 | solution.py:114
  90.2 2.0 fusion.118
  92.2 2.0 fusion.120
  94.2 2.0 fusion.122
  96.3 2.0 fusion.116
  98.3 2.0 fusion.118
  100.3 2.0 fusion.120
  102.4 2.0 fusion.122
  104.4 2.0 fusion.116
  106.5 2.0 fusion.118
  108.5 2.0 fusion.120
  110.5 2.0 fusion.122
  112.6 2.0 fusion.116
  114.6 2.0 fusion.118
  116.7 2.0 fusion.120
  120.7 2.0 fusion.116
  122.8 2.0 fusion.118
  124.8 2.0 fusion.120
  126.8 2.0 fusion.122
  128.9 2.0 fusion.116
  130.9 2.0 fusion.118
  133.0 2.0 fusion.120
  135.0 2.0 fusion.122
  137.1 2.0 fusion.116
  139.1 2.0 fusion.118
  143.2 2.0 fusion.122
  145.2 2.0 fusion.116
  147.2 2.0 fusion.118
  149.3 2.0 fusion.120
  151.3 2.0 fusion.122
  153.4 2.0 fusion.116
  161.5 2.0 fusion.116
  172.3 3.4 %all-to-all-start.1 = ((bf16[8,128,2,64]{1,3,2,0:T(8,128)(2,1)}), bf16[8,128,2,64]{1,3,2,0:T(8,128)(2,1)S(1)}, u32[]{:S(2)}, u32[]{:S(2)}) async-start(bf16[8,128,2,64]{1,3,2,0:T(8,128)(2,1)} %copy.30), calls=%async_computation.1 | async-start | bytes 524288 | tf_op jit(solution)/shard_map/all_to_all | solution.py:21
  175.8 3.8 %broadcast_select_fusion = bf16[128,16,1024]{2,1,0:T(8,128)(2,1)} fusion(bf16[128,16,1024]{2,1,0:T(8,128)(2,1)} %gather_fusion, pred[128,16]{1,0:T(8,128)(4,1)S(1)} %fusion.79), kind=kLoop, calls=%fused_computation.102 | loop fusion | flops 2097152 | bytes 8390656 | tf_op jit(solution)/shard_map/jit(_where)/select_n | solution.py:121
  179.6 10.4 %pmax.15 = f32[]{:T(128)} all-reduce(f32[]{:T(128)} %pmax.14), channel_id=1, replica_groups=mesh['tm'=8,'ep_0'=4,'ep_1'=4] {'ep_1'}, use_global_device_ids=true, to_apply=%region_5.6 | all-reduce | flops 1 | bytes 8 | tf_op jit(solution)/shard_map/pmax | solution.py:27
  190.0 7.4 %select_n.64 = bf16[16,8,16384]{2,1,0:T(8,128)(2,1)} reshape(bf16[128,16,1024]{2,1,0:T(8,128)(2,1)} %broadcast_select_fusion) | data formatting | bytes 8388608 | tf_op jit(solution)/shard_map/jit(_where)/select_n | solution.py:121
  198.6 2.4 pad_maximum_fusion
  201.0 53.7 %all_to_all.37 = bf16[16,8,16513]{2,1,0:T(8,128)(2,1)S(1)} all-to-all(bf16[16,8,16513]{2,1,0:T(8,128)(2,1)S(1)} %pad_maximum_fusion), channel_id=1, replica_groups=mesh['tm'=8,'ep_0'=4,'ep_1'=4] {'ep_0','ep_1'}, dimensions={0} | all-to-all | bytes 8454656 | tf_op jit(solution)/shard_map/all_to_all | solution.py:35
  257.5 7.5 %all-to-all-start.3 = ((bf16[8,128,2,64]{1,3,2,0:T(8,128)(2,1)}), bf16[8,128,2,64]{1,3,2,0:T(8,128)(2,1)S(1)}, u32[]{:S(2)}, u32[]{:S(2)}) async-start(bf16[8,128,2,64]{1,3,2,0:T(8,128)(2,1)} %broadcast_in_dim.32), calls=%async_computation.3 | async-start | bytes 524288 | tf_op jit(solution)/shard_map/all_to_all | solution.py:54
  265.0 2.5 slice.116
  267.5 4.8 %copy.39 = bf16[16,8,16,1024]{3,2,1,0:T(8,128)(2,1)} copy(bf16[16,8,16,1024]{3,1,2,0:T(8,128)(2,1)S(1)} %bitcast.65) | data formatting | bytes 8388608
  (89 shorter events, 31.1 us)
Async XLA Ops:
  0.6 1.6 copy-start
  5.1 6.1 %copy-start.5 = (s32[128]{0:T(128)S(1)}, s32[128]{0:T(128)}, u32[]{:S(2)}) copy-start(s32[128]{0:T(128)} %param.17) | copy-start | bytes 1540
  5.1 16.7 %copy-start.4 = (s32[128]{0:T(128)S(1)}, s32[128]{0:T(128)}, u32[]{:S(2)}) copy-start(s32[128]{0:T(128)} %param.16) | copy-start | bytes 1540
  5.1 54.9 %all-to-all-start = ((bf16[128,16,1024]{2,1,0:T(8,128)(2,1)}), bf16[128,16,1024]{2,1,0:T(8,128)(2,1)}, u32[]{:S(2)}, u32[]{:S(2)}) async-start(bf16[128,16,1024]{2,1,0:T(8,128)(2,1)} %gather_fusion), calls=%async_computation | async-start | bytes 8388608 | tf_op jit(solution)/shard_map/all_to_all | solution.py:99
  80.3 7.8 %copy-start.2 = (f32[2048]{0:T(1024)S(1)}, f32[2048]{0:T(1024)}, u32[]{:S(2)}) copy-start(f32[2048]{0:T(1024)} %param.13) | copy-start | bytes 24580
  80.3 7.8 %copy-start.3 = (f32[512]{0:T(512)S(1)}, f32[512]{0:T(512)}, u32[]{:S(2)}) copy-start(f32[512]{0:T(512)} %param.14) | copy-start | bytes 6148
  172.3 26.0 %all-to-all-start.1 = ((bf16[8,128,2,64]{1,3,2,0:T(8,128)(2,1)}), bf16[8,128,2,64]{1,3,2,0:T(8,128)(2,1)S(1)}, u32[]{:S(2)}, u32[]{:S(2)}) async-start(bf16[8,128,2,64]{1,3,2,0:T(8,128)(2,1)} %copy.30), calls=%async_computation.1 | async-start | bytes 524288 | tf_op jit(solution)/shard_map/all_to_all | solution.py:21
  254.6 2.0 copy-start.1
  257.5 16.1 %all-to-all-start.3 = ((bf16[8,128,2,64]{1,3,2,0:T(8,128)(2,1)}), bf16[8,128,2,64]{1,3,2,0:T(8,128)(2,1)S(1)}, u32[]{:S(2)}, u32[]{:S(2)}) async-start(bf16[8,128,2,64]{1,3,2,0:T(8,128)(2,1)} %broadcast_in_dim.32), calls=%async_computation.3 | async-start | bytes 524288 | tf_op jit(solution)/shard_map/all_to_all | solution.py:54
where the time goes:
time: 277 us; the launch traced here: 275 us
  matrix products  87.2 us (31%)
  blocking collectives  74 us (27%)
  local copies, waits for them, and re-layouts  46.9 us (17%)
  waiting for transfers between devices  37.9 us (14%)
  starting transfers between devices  17.1 us (6%)
  other arithmetic  10.3 us (4%)
    dot_general x40, matrix products, lstm_step(): jnp.dot(hidden.astype(jnp.bfloat16), hidden_weight, preferred_element_typ...  79.3 us
    all_to_all x1, blocking collectives, sent_together(): lax.all_to_all(both, axis, split_axis=split_dim, concat_axis=concat_dim,...  53.7 us
    all_to_all x1, waiting for transfers between devices, body(): lax.all_to_all(stored_rows, 'tm', split_axis=0, concat_axis=1, tiled=True)  37.9 us
    pmax x2, blocking collectives, one_axis_at_a_time(): x = lax.pmax(x, axis)  20.3 us
    gather x1, local copies, waits for them, and re-layouts, body(): burn_inputs = whole_slots[own_index, burn_steps]  15.3 us
    unnamed x14, local copies, waits for them, and re-layouts  8.41 us
    dot_general x1, matrix products, body(): jnp.dot(burn_inputs.reshape(BURN * own_count, burn_inputs.shape[2]), inpu...  7.84 us
    all_to_all x1, starting transfers between devices, sent_to_all(): return lax.all_to_all(copies, axis, split_axis=0, concat_axis=0, tiled=True)  7.54 us
  transfers between devices with their start and end apart: 3, of which 1 were waited for; matrix products, arithmetic and copies ran while one was open for 8% of the time, Pallas kernels for 0%

commit v1 on v0

--- a/solution.py
+++ b/solution.py
@@ -9,6 +9,18 @@
 UNROLL = 80
 EP = ("ep_0", "ep_1")
 IMPORTANCE = 0.6
+
+
+def cut_along(shard, dim, peers):
+    shape = shard.shape
+    blocks = shard.reshape(*shape[:dim], peers, shape[dim] // peers, *shape[dim + 1 :])
+    return jnp.moveaxis(blocks, dim, 0)
+
+
+def laid_out(blocks, dim):
+    shape = list(blocks.shape[1:])
+    shape[dim] *= blocks.shape[0]
+    return jnp.moveaxis(blocks, 0, dim).reshape(shape)
 
 
 def split_up(x, dim, devices):
@@ -96,7 +108,14 @@
     local_steps = position * shard_steps + jnp.arange(shard_steps, dtype=jnp.int32)
     offsets = (local_steps[None, :] - start_steps[:, None]) % STEPS
     own_count = seq_count // time_shards
-    whole_slots = lax.all_to_all(stored_rows, "tm", split_axis=0, concat_axis=1, tiled=True)
+    size, index = (lax.axis_size("tm"), lax.axis_index("tm"))
+    pieces = cut_along(stored_rows, 0, size)
+    finished = [pieces[index]]
+    for turn in range(1, size):
+        sent = pieces[index ^ turn]
+        finished.append(lax.ppermute(sent, "tm", [(i, i ^ turn) for i in range(size)]))
+    pieces = jnp.stack(finished)[index ^ jnp.arange(size)]
+    whole_slots = laid_out(pieces, 1)
     own_starts = lax.dynamic_slice_in_dim(start_steps, position * own_count, own_count)
     burn_steps = (own_starts[None, :] + jnp.arange(BURN, dtype=jnp.int32)[:, None]) % STEPS
     own_index = jnp.broadcast_to(jnp.arange(own_count, dtype=jnp.int32)[None, :], burn_steps.shape)

time: 277 us -> 265 us (0.957)
  matrix products: 87.2 us -> 59.7 us
  local copies, waits for them, and re-layouts: 46.9 us -> 58.1 us
  starting transfers between devices: 17.1 us -> 23.3 us
    ppermute x0 -> x7, waiting for transfers between devices: none -> 38.8 us  [body(): lax.ppermute(sent, 'tm', [(i, i ^ turn) for i in range(size)])]
    all_to_all x1 -> x0, waiting for transfers between devices: 37.9 us -> none  [body(): lax.all_to_all(stored_rows, 'tm', split_axis=0, concat_axis=1, tiled=True)]
    dot_general x40, matrix products: 79.3 us -> 51.8 us  [lstm_step(): jnp.dot(hidden.astype(jnp.bfloat16), hidden_weight, preferred_element_typ...]
    ppermute x0 -> x7, starting transfers between devices: none -> 11.4 us  [body(): lax.ppermute(sent, 'tm', [(i, i ^ turn) for i in range(size)])]
    all_to_all x1 -> x0, starting transfers between devices: 6.09 us -> none  [body(): lax.all_to_all(stored_rows, 'tm', split_axis=0, concat_axis=1, tiled=True)]
    unnamed x14 -> x24, local copies, waits for them, and re-layouts: 8.41 us -> 13.5 us
    all_to_all x1 -> x0, local copies, waits for them, and re-layouts: 4.99 us -> none  [body(): lax.all_to_all(stored_rows, 'tm', split_axis=0, concat_axis=1, tiled=True)]
    gather x0 -> x1, local copies, waits for them, and re-layouts: none -> 4.99 us  [body(): pieces = jnp.stack(finished)[index ^ jnp.arange(size)]]
  transfers between devices with their start and end apart: 3 -> 9, of which waited for: 1 -> 4; matrix products, arithmetic and copies ran while one was open for 8% -> 10% of each run, Pallas kernels for 0% -> 0%
where the time goes in v1:
time: 265 us; the launch traced here: 263 us
  blocking collectives  71.7 us (27%)
  matrix products  59.7 us (23%)
  local copies, waits for them, and re-layouts  58.1 us (22%)
  waiting for transfers between devices  38.8 us (15%)
  starting transfers between devices  23.3 us (9%)
  other arithmetic  10.3 us (4%)
    all_to_all x1, blocking collectives, sent_together(): lax.all_to_all(both, axis, split_axis=split_dim, concat_axis=concat_dim,...  51.9 us
    dot_general x40, matrix products, lstm_step(): jnp.dot(hidden.astype(jnp.bfloat16), hidden_weight, preferred_element_typ...  51.8 us
    ppermute x7, waiting for transfers between devices, body(): lax.ppermute(sent, 'tm', [(i, i ^ turn) for i in range(size)])  38.8 us
    pmax x2, blocking collectives, one_axis_at_a_time(): x = lax.pmax(x, axis)  19.8 us
    unnamed x24, local copies, waits for them, and re-layouts  13.5 us
    ppermute x7, starting transfers between devices, body(): lax.ppermute(sent, 'tm', [(i, i ^ turn) for i in range(size)])  11.4 us
    gather x1, local copies, waits for them, and re-layouts, body(): burn_inputs = whole_slots[own_index, burn_steps]  11.4 us
    dot_general x1, matrix products, body(): jnp.dot(burn_inputs.reshape(BURN * own_count, burn_inputs.shape[2]), inpu...  7.91 us
  transfers between devices with their start and end apart: 9, of which 4 were waited for; matrix products, arithmetic and copies ran while one was open for 10% of the time, Pallas kernels for 0%

profile of v1, /device:TPU:1, one launch (start us, length us, event | category | flops | bytes accessed | tf_op | source)
XLA Modules:
  0.0 263.3 jit_solution(10469053987465969795)
XLA Ops:
  2.2 2.8 %gather_fusion = bf16[128,16,1024]{2,1,0:T(8,128)(2,1)} fusion(bf16[64,16,1024]{2,1,0:T(8,128)(2,1)S(1)} %copy-done, s32[1024]{0:T(1024)S(1)} %pad_clamp_fusion.1), kind=kCustom, calls=%fused_computation | custom fusion | bytes 8389120 | tf_op jit(solution)/shard_map/gather | solution.py:107
  5.1 4.3 %dynamic-slice_bitcast_fusion.4 = (bf16[16,16,1024]{2,1,0:T(8,128)(2,1)}, bf16[16,16,1024]{2,1,0:T(8,128)(2,1)}, bf16[16,16,1024]{2,1,0:T(8,128)(2,1)}, bf16[16,...) fusion(bf16[8,16,16,1024]{3,2,1,0:T(8,128)(2,1)} %bitcast.91, ...), kind=kLoop, calls=%fused_computation.111 | loop fusion | bytes 8388640 | tf_op jit(solution)/shard_map/squeeze | solution.py:115
  9.3 1.4 collective-permute-start
  10.7 1.4 collective-permute-start.1
  12.4 3.0 %collective-permute-start.3 = (bf16[16,16,1024]{2,1,0:T(8,128)(2,1)}, bf16[16,16,1024]{2,1,0:T(8,128)(2,1)S(1)}, u32[]{:S(2)}, u32[]{:S(2)}) collective-permute-start(bf16[16,16,1024]{2,1,0:T(8,128)(2,1)} %get-tuple-element.95), channel_id=1, source_target_pairs={{0,64},{16,80},{32,96},{48,112},{64,0},{80,16},{96,32},{112,48},{1... | collective-permute-start | bytes 1572872 | tf_op jit(solution)/shard_map/ppermute | solution.py:116
  16.6 9.3 %pmax.14 = f32[]{:T(128)} all-reduce(bf16[]{:T(256)} %convert_reduce_fusion), channel_id=1, replica_groups=mesh['tm'=8,'ep_0'=4,'ep_1'=4] {'ep_0'}, use_global_device_ids=true, to_apply=%region_4.5 | all-reduce | flops 1 | bytes 6 | tf_op jit(solution)/shard_map/pmax | solution.py:39
  26.0 2.8 %collective-permute-start.5 = (bf16[16,16,1024]{2,1,0:T(8,128)(2,1)}, bf16[16,16,1024]{2,1,0:T(8,128)(2,1)S(1)}, u32[]{:S(2)}, u32[]{:S(2)}) collective-permute-start(bf16[16,16,1024]{2,1,0:T(8,128)(2,1)} %get-tuple-element.93), channel_id=1, source_target_pairs={{0,96},{16,112},{32,64},{48,80},{64,32},{80,48},{96,0},{112,16},{1... | collective-permute-start | bytes 1572872 | tf_op jit(solution)/shard_map/ppermute | solution.py:116
  29.6 2.2 collective-permute-start.6
  32.7 4.0 %collective-permute-done.2 = bf16[16,16,1024]{2,1,0:T(8,128)(2,1)S(1)} collective-permute-done((bf16[16,16,1024]{2,1,0:T(8,128)(2,1)}, bf16[16,16,1024]{2,1,0:T(8,128)(2,1)S(1)}, u32[]{:S(2)}, u32[]{:S(2)}) %collective-permute-start.2) | collective-permute-done | bytes 524320 | tf_op jit(solution)/shard_map/ppermute | solution.py:116
  37.5 11.9 %collective-permute-done.3 = bf16[16,16,1024]{2,1,0:T(8,128)(2,1)S(1)} collective-permute-done((bf16[16,16,1024]{2,1,0:T(8,128)(2,1)}, bf16[16,16,1024]{2,1,0:T(8,128)(2,1)S(1)}, u32[]{:S(2)}, u32[]{:S(2)}) %collective-permute-start.3) | collective-permute-done | bytes 524320 | tf_op jit(solution)/shard_map/ppermute | solution.py:116
  50.3 10.7 %collective-permute-done.4 = bf16[16,16,1024]{2,1,0:T(8,128)(2,1)S(1)} collective-permute-done((bf16[16,16,1024]{2,1,0:T(8,128)(2,1)}, bf16[16,16,1024]{2,1,0:T(8,128)(2,1)S(1)}, u32[]{:S(2)}, u32[]{:S(2)}) %collective-permute-start.4) | collective-permute-done | bytes 524320 | tf_op jit(solution)/shard_map/ppermute | solution.py:116
  62.6 12.2 %collective-permute-done.6 = bf16[16,16,1024]{2,1,0:T(8,128)(2,1)S(1)} collective-permute-done((bf16[16,16,1024]{2,1,0:T(8,128)(2,1)}, bf16[16,16,1024]{2,1,0:T(8,128)(2,1)S(1)}, u32[]{:S(2)}, u32[]{:S(2)}) %collective-permute-start.6) | collective-permute-done | bytes 524320 | tf_op jit(solution)/shard_map/ppermute | solution.py:116
  75.7 5.0 %gather_fusion.1 = bf16[8,16,16,1024]{3,2,1,0:T(8,128)(2,1)} fusion(bf16[8,16,16,1024]{3,2,1,0:T(8,128)(2,1)} %bitcast_dynamic-update-slice_fusion, s32[1024]{0:T(1024)S(1)} %pad_clamp_fusion), kind=kCustom, calls=%fused_computation.1 | custom fusion | bytes 8388640 | tf_op jit(solution)/shard_map/gather | solution.py:117
  80.7 5.0 %copy.26 = bf16[16,8,16,1024]{3,2,1,0:T(8,128)(2,1)} copy(bf16[16,8,16,1024]{3,2,0,1:T(8,128)(2,1)} %bitcast.95) | data formatting | bytes 8388608 | tf_op jit(solution)/shard_map/transpose | solution.py:23
  85.7 11.4 %gather_fusion.2 = bf16[640,1024]{1,0:T(8,128)(2,1)} fusion(bf16[16,128,1024]{2,1,0:T(8,128)(2,1)} %bitcast.90, s32[640]{0:T(1024)S(1)} %reshape.231), kind=kCustom, calls=%fused_computation.2 | custom fusion | bytes 2626560 | tf_op jit(solution)/shard_map/gather | solution.py:122
  97.0 7.9 %fusion.75 = f32[10,4,16,2048]{3,2,1,0:T(8,128)} fusion(bf16[10,4,16,1024]{3,2,1,0:T(8,128)(2,1)} %bitcast.98, bf16[1024,2048]{1,0:T(8,128)(2,1)} %param.11), kind=kOutput, calls=%fused_computation.101 | convolution fusion | flops 2684354560 | bytes 10747904 | tf_op jit(solution)/shard_map/dot_general | solution.py:123
  105.0 54.0 %while.13 = (s32[]{:T(128)}, bf16[16,512]{1,0:T(8,128)(2,1)S(1)}, f32[16,512]{1,0:T(8,128)S(1)}, f32[10,4,16,2048]{3,2,1,0:T(8,128)}, bf16[512,2048]{1,0:T(8,128...) while((s32[]{:T(128)}, bf16[16,512]{1,0:T(8,128)(2,1)S(1)}, ...), condition=%wide.region_1.2_spmd.clone, body=%wide.region_0.1_spmd.clone.sunk | while | flops 134987776 | bytes 10395840 | solution.py:133
  105.0 1.3 fusion.117
  106.3 1.3 fusion.119
  107.7 1.3 fusion.121
  109.0 1.3 fusion.123
  110.4 1.3 fusion.117
  111.7 1.3 fusion.119
  113.1 1.3 fusion.121
  114.4 1.3 fusion.123
  115.8 1.3 fusion.117
  117.1 1.3 fusion.119
  119.8 1.3 fusion.123
  121.2 1.3 fusion.117
  122.5 1.3 fusion.119
  126.6 1.3 fusion.117
  132.0 1.3 fusion.117
  137.4 1.3 fusion.117
  142.8 1.3 fusion.117
  148.2 1.3 fusion.117
  153.6 1.3 fusion.117
  159.2 1.7 dynamic_update_slice.3
  161.6 4.3 %all-to-all-start = ((bf16[8,128,2,64]{1,3,2,0:T(8,128)(2,1)}), bf16[8,128,2,64]{1,3,2,0:T(8,128)(2,1)S(1)}, u32[]{:S(2)}, u32[]{:S(2)}) async-start(bf16[8,128,2,64]{1,3,2,0:T(8,128)(2,1)} %copy.28), calls=%async_computation | async-start | bytes 524288 | tf_op jit(solution)/shard_map/all_to_all | solution.py:33
  166.0 3.8 %broadcast_select_fusion = bf16[128,16,1024]{2,1,0:T(8,128)(2,1)} fusion(bf16[128,16,1024]{2,1,0:T(8,128)(2,1)} %gather_fusion, pred[128,16]{1,0:T(8,128)(4,1)S(1)} %fusion.79), kind=kLoop, calls=%fused_computation.103 | loop fusion | flops 2097152 | bytes 8390656 | tf_op jit(solution)/shard_map/jit(_where)/select_n | solution.py:140
  169.8 10.6 %pmax.15 = f32[]{:T(128)} all-reduce(f32[]{:T(128)} %pmax.14), channel_id=1, replica_groups=mesh['tm'=8,'ep_0'=4,'ep_1'=4] {'ep_1'}, use_global_device_ids=true, to_apply=%region_5.6 | all-reduce | flops 1 | bytes 8 | tf_op jit(solution)/shard_map/pmax | solution.py:39
  180.4 7.4 %select_n.98 = bf16[16,8,16384]{2,1,0:T(8,128)(2,1)} reshape(bf16[128,16,1024]{2,1,0:T(8,128)(2,1)} %broadcast_select_fusion) | data formatting | bytes 8388608 | tf_op jit(solution)/shard_map/jit(_where)/select_n | solution.py:140
  188.9 2.4 pad_maximum_fusion
  191.3 51.9 %all_to_all.19 = bf16[16,8,16513]{2,1,0:T(8,128)(2,1)S(1)} all-to-all(bf16[16,8,16513]{2,1,0:T(8,128)(2,1)S(1)} %pad_maximum_fusion), channel_id=1, replica_groups=mesh['tm'=8,'ep_0'=4,'ep_1'=4] {'ep_0','ep_1'}, dimensions={0} | all-to-all | bytes 8454656 | tf_op jit(solution)/shard_map/all_to_all | solution.py:47
  243.2 2.0 copy-done.3
  246.1 7.6 %all-to-all-start.2 = ((bf16[8,128,2,64]{1,3,2,0:T(8,128)(2,1)}), bf16[8,128,2,64]{1,3,2,0:T(8,128)(2,1)S(1)}, u32[]{:S(2)}, u32[]{:S(2)}) async-start(bf16[8,128,2,64]{1,3,2,0:T(8,128)(2,1)} %broadcast_in_dim.32), calls=%async_computation.2 | async-start | bytes 524288 | tf_op jit(solution)/shard_map/all_to_all | solution.py:66
  253.7 2.5 slice.118
  256.2 4.8 %copy.37 = bf16[16,8,16,1024]{3,2,1,0:T(8,128)(2,1)} copy(bf16[16,8,16,1024]{3,1,2,0:T(8,128)(2,1)S(1)} %bitcast.96) | data formatting | bytes 8388608
  261.0 1.4 slice_reduce_fusion
  (116 shorter events, 41.8 us)
Async XLA Ops:
  0.6 1.6 copy-start
  5.1 10.7 %copy-start.6 = (s32[128]{0:T(128)S(1)}, s32[128]{0:T(128)}, u32[]{:S(2)}) copy-start(s32[128]{0:T(128)} %param.16) | copy-start | bytes 1540
  5.1 10.9 %copy-start.7 = (s32[128]{0:T(128)S(1)}, s32[128]{0:T(128)}, u32[]{:S(2)}) copy-start(s32[128]{0:T(128)} %param.17) | copy-start | bytes 1540
  9.3 16.6 %collective-permute-start = (bf16[16,16,1024]{2,1,0:T(8,128)(2,1)}, bf16[16,16,1024]{2,1,0:T(8,128)(2,1)S(1)}, u32[]{:S(2)}, u32[]{:S(2)}) collective-permute-start(bf16[16,16,1024]{2,1,0:T(8,128)(2,1)} %get-tuple-element.98), channel_id=1, source_target_pairs={{0,16},{16,0},{32,48},{48,32},{64,80},{80,64},{96,112},{112,96},{1... | collective-permute-start | bytes 1572872 | tf_op jit(solution)/shard_map/ppermute | solution.py:116
  10.7 18.9 %collective-permute-start.1 = (bf16[16,16,1024]{2,1,0:T(8,128)(2,1)}, bf16[16,16,1024]{2,1,0:T(8,128)(2,1)S(1)}, u32[]{:S(2)}, u32[]{:S(2)}) collective-permute-start(bf16[16,16,1024]{2,1,0:T(8,128)(2,1)} %get-tuple-element.97), channel_id=1, source_target_pairs={{0,32},{16,48},{32,0},{48,16},{64,96},{80,112},{96,64},{112,80},{1... | collective-permute-start | bytes 1572872 | tf_op jit(solution)/shard_map/ppermute | solution.py:116
  12.1 24.5 %collective-permute-start.2 = (bf16[16,16,1024]{2,1,0:T(8,128)(2,1)}, bf16[16,16,1024]{2,1,0:T(8,128)(2,1)S(1)}, u32[]{:S(2)}, u32[]{:S(2)}) collective-permute-start(bf16[16,16,1024]{2,1,0:T(8,128)(2,1)} %get-tuple-element.96), channel_id=1, source_target_pairs={{0,48},{16,32},{32,16},{48,0},{64,112},{80,96},{96,80},{112,64},{1... | collective-permute-start | bytes 1572872 | tf_op jit(solution)/shard_map/ppermute | solution.py:116
  12.4 37.0 %collective-permute-start.3 = (bf16[16,16,1024]{2,1,0:T(8,128)(2,1)}, bf16[16,16,1024]{2,1,0:T(8,128)(2,1)S(1)}, u32[]{:S(2)}, u32[]{:S(2)}) collective-permute-start(bf16[16,16,1024]{2,1,0:T(8,128)(2,1)} %get-tuple-element.95), channel_id=1, source_target_pairs={{0,64},{16,80},{32,96},{48,112},{64,0},{80,16},{96,32},{112,48},{1... | collective-permute-start | bytes 1572872 | tf_op jit(solution)/shard_map/ppermute | solution.py:116
  15.5 45.5 %collective-permute-start.4 = (bf16[16,16,1024]{2,1,0:T(8,128)(2,1)}, bf16[16,16,1024]{2,1,0:T(8,128)(2,1)S(1)}, u32[]{:S(2)}, u32[]{:S(2)}) collective-permute-start(bf16[16,16,1024]{2,1,0:T(8,128)(2,1)} %get-tuple-element.94), channel_id=1, source_target_pairs={{0,80},{16,64},{32,112},{48,96},{64,16},{80,0},{96,48},{112,32},{1... | collective-permute-start | bytes 1572872 | tf_op jit(solution)/shard_map/ppermute | solution.py:116
  26.0 35.8 %collective-permute-start.5 = (bf16[16,16,1024]{2,1,0:T(8,128)(2,1)}, bf16[16,16,1024]{2,1,0:T(8,128)(2,1)S(1)}, u32[]{:S(2)}, u32[]{:S(2)}) collective-permute-start(bf16[16,16,1024]{2,1,0:T(8,128)(2,1)} %get-tuple-element.93), channel_id=1, source_target_pairs={{0,96},{16,112},{32,64},{48,80},{64,32},{80,48},{96,0},{112,16},{1... | collective-permute-start | bytes 1572872 | tf_op jit(solution)/shard_map/ppermute | solution.py:116
  29.6 45.3 %collective-permute-start.6 = (bf16[16,16,1024]{2,1,0:T(8,128)(2,1)}, bf16[16,16,1024]{2,1,0:T(8,128)(2,1)S(1)}, u32[]{:S(2)}, u32[]{:S(2)}) collective-permute-start(bf16[16,16,1024]{2,1,0:T(8,128)(2,1)} %get-tuple-element.92), channel_id=1, source_target_pairs={{0,112},{16,96},{32,80},{48,64},{64,48},{80,32},{96,16},{112,0},{1... | collective-permute-start | bytes 1572872 | tf_op jit(solution)/shard_map/ppermute | solution.py:116
  97.0 7.9 %copy-start.2 = (bf16[512,2048]{1,0:T(8,128)(2,1)S(1)}, bf16[512,2048]{1,0:T(8,128)(2,1)}, u32[]{:S(2)}) copy-start(bf16[512,2048]{1,0:T(8,128)(2,1)} %param.12) | copy-start | bytes 6291460
  97.0 7.9 %copy-start.4 = (f32[2048]{0:T(1024)S(1)}, f32[2048]{0:T(1024)}, u32[]{:S(2)}) copy-start(f32[2048]{0:T(1024)} %param.13) | copy-start | bytes 24580
  97.0 7.9 %copy-start.5 = (f32[512]{0:T(512)S(1)}, f32[512]{0:T(512)}, u32[]{:S(2)}) copy-start(f32[512]{0:T(512)} %param.14) | copy-start | bytes 6148
  161.6 27.0 %all-to-all-start = ((bf16[8,128,2,64]{1,3,2,0:T(8,128)(2,1)}), bf16[8,128,2,64]{1,3,2,0:T(8,128)(2,1)S(1)}, u32[]{:S(2)}, u32[]{:S(2)}) async-start(bf16[8,128,2,64]{1,3,2,0:T(8,128)(2,1)} %copy.28), calls=%async_computation | async-start | bytes 524288 | tf_op jit(solution)/shard_map/all_to_all | solution.py:33
  243.2 2.0 copy-start.3
  246.1 16.3 %all-to-all-start.2 = ((bf16[8,128,2,64]{1,3,2,0:T(8,128)(2,1)}), bf16[8,128,2,64]{1,3,2,0:T(8,128)(2,1)S(1)}, u32[]{:S(2)}, u32[]{:S(2)}) async-start(bf16[8,128,2,64]{1,3,2,0:T(8,128)(2,1)} %broadcast_in_dim.32), calls=%async_computation.2 | async-start | bytes 524288 | tf_op jit(solution)/shard_map/all_to_all | solution.py:66
  256.2 7.1 %copy-start.1 = (bf16[64,16,1024]{2,1,0:T(8,128)(2,1)S(1)}, bf16[64,16,1024]{2,1,0:T(8,128)(2,1)}, u32[]{:S(2)}) copy-start(bf16[64,16,1024]{2,1,0:T(8,128)(2,1)} %param.10) | copy-start | bytes 6291460
